TPU v7x, 128 devices: a whole 4x4x4 slice. The times are simulated.
128 devices in a mesh: member: 8 (over x, core), region: 16 (over z, y).
Axes of the slice: x: 4, y: 4, z: 4, core: 2. Of those that a mesh axis runs over, the one named last changes fastest.
Arguments:
- ensemble: float32 [24, 32, 128, 512], P('member', 'region'), may hold values from -6 to 6
- obs_value: float32 [32, 128, 128], P(None, ('member', 'region')), may hold values from -6 to 6
- obs_error: float32 [32, 128, 128], P(None, ('member', 'region')), may hold values from 0.5 to 4
- obs_index: int32 [32, 128, 128], P(None, ('member', 'region')), may hold values from 0 to 511
- obs_count: int32 [32, 128], P(None, ('member', 'region')), may hold values from 1 to 128
Outputs:
- analysis: float32 [24, 32, 128, 512], P('member', 'region')
Inputs may be any that keep to these rules, and one draw needn't show every extreme that they name: `obs_index`: value v names field v // (256) (0 SST, 1 SSH) at cell v mod (256) of the block, cells row-major. `obs_count`: slots below a block's count are observations; the others are padding and carry no weight.
All inputs are finite; a program needn't handle non-finite values.
Results may differ from a plain program's by a relative error of at most 0.0001.
Values sent between devices are 32-bit elements; how exact they have to be, the bound alone decides.
A program may use at most 64 MiB of HBM per device.

v0:
```python
import functools
import math

import jax
import jax.numpy as jnp
from jax import lax
from jax.experimental import pallas as pl
from jax.experimental.pallas import tpu as pltpu
from jax.sharding import PartitionSpec as P

SIDE = 16
CELLS = SIDE * SIDE
HALF = SIDE // 2
LANES = 128
NS_ITERS = 6
LOC_SCALE = 12.0
INFLATION_FACTOR = 1.1
MESH = pl.DeviceIdType.MESH
NT = (((1,), (1,)), ((), ()))


def up_to(value, step):
    return -(-value // step) * step


def split(values):
    high = values.astype(jnp.bfloat16)
    low = (values - high.astype(jnp.float32)).astype(jnp.bfloat16)
    return high, low


def kernel(
    dims,
    ens_ref, value_any, error_any, index_any, count_ref, out_ref,
    value_ref, error_ref, index_ref, ens, pack, obs, mean, slots, place, loc, qhi, qlo, acc, side,
    row_in, side_in, prec, root, inv, step, small, weights, outgoing,
    ens_send, ens_recv, obs_send, obs_recv, halo_send, halo_recv, out_send, out_recv, local_sem,
):
    M, G, K, R, C, V, O, J, QP = dims
    members = M * K
    m = lax.axis_index("member")
    g = lax.axis_index("region")
    pack_rows = pack.shape[0] // G
    ts = 2 * (R + 2)
    targets = 4 * C * (R + 2)
    f32 = jnp.float32

    loads = []
    for n, (src, dst) in enumerate(((value_any, value_ref), (error_any, error_ref), (index_any, index_ref))):
        load = pltpu.make_async_copy(src, dst, local_sem.at[3 + n])
        load.start()
        loads.append(load)
    barrier = pltpu.get_barrier_semaphore()
    for off in range(1, M):
        pl.semaphore_signal(barrier, inc=1, device_id=(lax.rem(m + off, M), g), device_id_type=MESH)
    for off in range(1, G):
        pl.semaphore_signal(barrier, inc=1, device_id=(m, lax.rem(g + off, G)), device_id_type=MESH)
    near = {}
    for dm in (-1, 0, 1):
        for dg in (-1, 0, 1):
            if dm == 0 and dg == 0:
                continue
            ok = jnp.bool_(True)
            if dm:
                ok = jnp.logical_and(ok, m > 0 if dm < 0 else m < M - 1)
            if dg:
                ok = jnp.logical_and(ok, g > 0 if dg < 0 else g < G - 1)
            near[dm, dg] = ok
            if dm and dg:
                @pl.when(ok)
                def _():
                    pl.semaphore_signal(barrier, inc=1, device_id=(m + dm, g + dg), device_id_type=MESH)

    own_ens = pltpu.make_async_copy(
        ens_ref.at[:, :, pl.ds(pl.multiple_of(m * C, C), C), :], ens.at[pl.ds(m * K, K)], local_sem.at[0]
    )
    own_ens.start()
    for load in loads:
        load.wait()
    slot = lax.broadcasted_iota(jnp.int32, (G * R, O), 1)
    slot_row = lax.broadcasted_iota(jnp.int32, (G * R, O), 0)
    count = jnp.zeros((G * R, O), jnp.int32)
    for d in range(G * R):
        count = jnp.where(slot_row == d, count_ref[0, d], count)
    live = jnp.where(slot < count, 1.0, 0.0).astype(f32)
    weight = jnp.sqrt(live / error_ref[...])
    value = value_ref[...]
    index_f = index_ref[...].astype(f32)
    for d in range(G):
        base = d * pack_rows
        pack[base : base + R, :] = weight[d * R : (d + 1) * R]
        pack[base + R : base + 2 * R, :] = value[d * R : (d + 1) * R]
        pack[base + 2 * R : base + 3 * R, :] = index_f[d * R : (d + 1) * R]
        if pack_rows > 3 * R:
            pack[base + 3 * R : base + pack_rows, :] = jnp.zeros((pack_rows - 3 * R, O), f32)
    if QP > members * J:
        qhi[members * J :, :] = jnp.zeros((QP - members * J, qhi.shape[1]), jnp.bfloat16)
        qlo[members * J :, :] = jnp.zeros((QP - members * J, qlo.shape[1]), jnp.bfloat16)

    sides = jnp.where(m > 0, 1, 0) + jnp.where(m < M - 1, 1, 0)
    ends = jnp.where(g > 0, 1, 0) + jnp.where(g < G - 1, 1, 0)
    pl.semaphore_wait(barrier, M - 1 + G - 1 + sides * ends)

    sends = []
    for off in range(1, M):
        to = lax.rem(m + off, M)
        copy = pltpu.make_async_remote_copy(
            src_ref=ens_ref.at[:, :, pl.ds(pl.multiple_of(to * C, C), C), :],
            dst_ref=ens.at[pl.ds(m * K, K)],
            send_sem=ens_send.at[off], recv_sem=ens_recv.at[off],
            device_id=(to, g), device_id_type=MESH,
        )
        copy.start()
        sends.append(copy)
    own_row = pl.ds(pl.multiple_of(g * pack_rows, pack_rows), pack_rows)
    own_obs = pltpu.make_async_copy(pack.at[own_row], obs.at[own_row], local_sem.at[1])
    own_obs.start()
    for off in range(1, G):
        to = lax.rem(g + off, G)
        copy = pltpu.make_async_remote_copy(
            src_ref=pack.at[pl.ds(pl.multiple_of(to * pack_rows, pack_rows), pack_rows)],
            dst_ref=obs.at[own_row],
            send_sem=obs_send.at[off], recv_sem=obs_recv.at[off],
            device_id=(m, to), device_id_type=MESH,
        )
        copy.start()
        sends.append(copy)
    own_ens.wait()
    own_obs.wait()
    for off in range(1, M):
        came = lax.rem(m + M - off, M)
        pltpu.make_async_remote_copy(
            src_ref=ens_ref.at[:, :, pl.ds(pl.multiple_of(m * C, C), C), :],
            dst_ref=ens.at[pl.ds(came * K, K)],
            send_sem=ens_send.at[off], recv_sem=ens_recv.at[off],
            device_id=(came, g), device_id_type=MESH,
        ).wait_recv()
    for off in range(1, G):
        came = lax.rem(g + G - off, G)
        pltpu.make_async_remote_copy(
            src_ref=pack.at[own_row],
            dst_ref=obs.at[pl.ds(pl.multiple_of(came * pack_rows, pack_rows), pack_rows)],
            send_sem=obs_send.at[off], recv_sem=obs_recv.at[off],
            device_id=(m, came), device_id_type=MESH,
        ).wait_recv()

    tiles = V // LANES
    for i in range(R):
        wgt = obs[pl.ds(i, C, stride=pack_rows), :]
        val = obs[pl.ds(R + i, C, stride=pack_rows), :]
        idx = obs[pl.ds(2 * R + i, C, stride=pack_rows), :].astype(jnp.int32)
        lane = idx & (LANES - 1)
        tile = idx >> 7
        cell = idx & (CELLS - 1)
        place[2 * i] = (cell >> 4).astype(f32)
        place[2 * i + 1] = (cell & (SIDE - 1)).astype(f32)

        def seen(rows):
            got = jnp.take_along_axis(rows[:, :LANES], lane, axis=1)
            for t in range(1, tiles):
                more = jnp.take_along_axis(rows[:, t * LANES : (t + 1) * LANES], lane, axis=1)
                got = jnp.where(tile == t, more, got)
            return got

        total = ens[0, i]
        for k in range(1, members):
            total = total + ens[k, i]
        avg = total * (1.0 / members)
        mean[i] = avg
        seen_mean = seen(avg)
        base = i * J * C
        for k in range(members):
            slots[base + k * C : base + (k + 1) * C, :] = wgt * (seen(ens[k, i]) - seen_mean)
        slots[base + members * C : base + (members + 1) * C, :] = wgt * (val - seen_mean)
        if J > members + 1:
            slots[base + (members + 1) * C : base + J * C, :] = jnp.zeros(((J - members - 1) * C, O), f32)

    scale = -1.0 / (2.0 * LOC_SCALE * LOC_SCALE)
    middle = (HALF - 1) * 0.5
    t_id = lax.broadcasted_iota(jnp.int32, (ts, O), 0)
    t_row = t_id >> 1
    t_mid = (t_id & 1).astype(f32) * HALF + middle
    col = lax.broadcasted_iota(jnp.int32, (C, O), 0)
    edges = {0: [None] * R, 1: [None] * R}
    for c in range(C):
        for i in range(R):
            at = (c * R + i) * O
            here = slots[pl.ds(i * J * C + c, J, stride=C), :]
            prod = jnp.concatenate([here[k : k + 1] * here for k in range(members)], axis=0)
            high, low = split(prod)
            qhi[0 : members * J, at : at + O] = high
            qlo[0 : members * J, at : at + O] = low
            y = place[2 * i, c : c + 1, :]
            x = place[2 * i + 1, c : c + 1, :]
            row_off = i + 1 - t_row
            dy = (row_off * SIDE).astype(f32) + y - t_mid
            ly = jnp.where(jnp.abs(row_off) <= 1, jnp.exp(dy * dy * scale), 0.0)
            col_off = c - col
            lx = []
            for pc in range(2):
                dx = (col_off * SIDE).astype(f32) + x - (pc * HALF + middle)
                lx.append(jnp.where(jnp.abs(col_off) <= 1, jnp.exp(dx * dx * scale), 0.0))
            grid = jnp.concatenate([ly[s : s + 1] * lx[pc] for s in range(ts) for pc in range(2)], axis=0)
            high, low = split(grid)
            loc[0:targets, at : at + O] = high
            loc[targets : 2 * targets, at : at + O] = low
            for which, away, at_col in ((0, 1, 0), (1, -1, C - 1)):
                if c == at_col:
                    parts = []
                    for pc in range(2):
                        dx = away * SIDE + x - (pc * HALF + middle)
                        parts.append(ly * jnp.exp(dx * dx * scale))
                    edges[which][i] = jnp.concatenate(parts, axis=0)

    def dot(left, right):
        return lax.dot_general(left, right, NT, preferred_element_type=f32)

    for which, first in ((0, 0), (1, (C - 1) * R * O)):
        high, low = split(jnp.concatenate(edges[which], axis=1))
        hq = qhi[:, first : first + R * O]
        side[which] = dot(high, hq) + dot(low, hq) + dot(high, qlo[:, first : first + R * O])
    both = dot(loc[...], qhi[...])
    acc[...] = both[:targets] + both[targets:] + dot(loc[0:targets, :], qlo[...])

    rows = 4 * C
    plans = []
    for n, (dm, dg) in enumerate(near):
        if dm == 0:
            first = 0 if dg < 0 else (R + 1) * rows
            src = acc.at[first : first + rows]
            dst = row_in.at[0 if dg < 0 else 1]
        else:
            src = side.at[0 if dm < 0 else 1]
            dst = side_in.at[(0 if dm < 0 else 3) + dg + 1]
        plans.append((dm, dg, src, dst, n))
    for dm, dg, src, dst, n in plans:
        @pl.when(near[dm, dg])
        def _():
            pltpu.make_async_remote_copy(
                src_ref=src, dst_ref=dst, send_sem=halo_send.at[n], recv_sem=halo_recv.at[n],
                device_id=(m + dm, g + dg), device_id_type=MESH,
            ).start()
    for dm, dg, src, dst, n in plans:
        @pl.when(near[-dm, -dg])
        def _():
            pltpu.make_async_remote_copy(
                src_ref=src, dst_ref=dst, send_sem=halo_send.at[n], recv_sem=halo_recv.at[n],
                device_id=(m - dm, g - dg), device_id_type=MESH,
            ).wait_recv()

        @pl.when(jnp.logical_not(near[-dm, -dg]))
        def _():
            dst[...] = jnp.zeros(dst.shape, f32)

    sub = lax.broadcasted_iota(jnp.int32, (C, QP), 0)
    own = R * rows
    for i in range(R):
        for pr in range(2):
            for pc in range(2):
                first = (i * 4 + pr * 2 + pc) * C
                block = acc[rows + first : rows + first + C, :]
                if i == R - 1:
                    block = block + row_in[0, (pr * 2 + pc) * C : (pr * 2 + pc + 1) * C, :]
                if i == 0:
                    block = block + row_in[1, (pr * 2 + pc) * C : (pr * 2 + pc + 1) * C, :]
                for base, at_col in ((0, C - 1), (3, 0)):
                    def pick(dg, t):
                        place_in = pc * ts + t * 2 + pr
                        return side_in[base + dg + 1, place_in : place_in + 1, :]

                    line = pick(0, i + 1)
                    if i == R - 1:
                        line = line + pick(-1, 0)
                    if i == 0:
                        line = line + pick(1, R + 1)
                    block = block + jnp.where(sub == at_col, line, 0.0)
                prec[first : first + C, :] = block
    width = prec.shape[0]
    if width > own:
        prec[own:, :] = jnp.zeros((width - own, QP), f32)

    flat = jnp.transpose(prec[...])
    j_id = lax.broadcasted_iota(jnp.int32, (J, width), 0)
    eye = [jnp.where(j_id == k, 1.0, 0.0).astype(f32) for k in range(members)]
    drive = []
    mats = []
    squares = None
    for k in range(members):
        line = flat[k * J : (k + 1) * J]
        drive.append(line[members : members + 1])
        mat = jnp.where(j_id < members, line, 0.0) + ((members - 1) / INFLATION_FACTOR) * eye[k]
        mats.append(mat)
        squares = mat * mat if squares is None else squares + mat * mat
    norm = jnp.sqrt(jnp.sum(squares, axis=0, keepdims=True))
    for k in range(members):
        start = mats[k] / norm
        first_m = 1.5 * eye[k] - 0.5 * start
        root[k] = start
        step[k] = first_m
        inv[k] = first_m

    def times(left, k, right):
        out = left[k, 0:1, :] * right[0]
        for i in range(1, members):
            out = out + left[k, i : i + 1, :] * right[i]
        return out

    def apply(*lefts):
        right = [step[i] for i in range(members)]
        for k in range(members):
            for left in lefts:
                left[k] = times(left, k, right)

    def next_step():
        right = [root[i] for i in range(members)]
        for k in range(members):
            step[k] = 1.5 * jnp.where(j_id == k, 1.0, 0.0) - 0.5 * times(inv, k, right)

    apply(root)

    def sweep(_, carry):
        next_step()
        apply(root, inv)
        return carry

    lax.fori_loop(0, NS_ITERS - 2, sweep, 0)
    next_step()
    apply(inv)
    shrink = 1.0 / jnp.sqrt(norm)
    inv_root = [inv[k] * shrink for k in range(members)]
    half_way = drive[0] * inv_root[0]
    for i in range(1, members):
        half_way = half_way + drive[i] * inv_root[i]
    small[0] = half_way
    mean_w = small[0, 0:1, :] * inv_root[0]
    for i in range(1, members):
        mean_w = mean_w + small[0, i : i + 1, :] * inv_root[i]
    small[1] = mean_w
    for j in range(members):
        weights[j * J : (j + 1) * J, :] = small[1, j : j + 1, :] + math.sqrt(members - 1) * inv_root[j]
    if QP > members * J:
        weights[members * J :, :] = jnp.zeros((QP - members * J, width), f32)
    prec[...] = jnp.transpose(weights[...])

    fields = V // CELLS
    band = HALF * SIDE
    left_half = (lax.broadcasted_iota(jnp.int32, (C, band), 1) & (SIDE - 1)) < HALF
    def update(dest):
        for i in range(R):
            for h in range(2):
                first = (i * 4 + 2 * h) * C
                west = prec[first : first + C, :]
                east = prec[first + C : first + 2 * C, :]
                lanes = [f * CELLS + h * band for f in range(fields)]
                avgs = [mean[i, :, a : a + band] for a in lanes]
                outs = [[avgs[f] for f in range(fields)] for _ in range(K)]
                for j in range(members):
                    anoms = [ens[j, i, :, a : a + band] - avgs[f] for f, a in enumerate(lanes)]
                    for kk in range(K):
                        q = j * J + dest * K + kk
                        w = jnp.where(
                            left_half,
                            jnp.broadcast_to(west[:, q : q + 1], (C, band)),
                            jnp.broadcast_to(east[:, q : q + 1], (C, band)),
                        )
                        for f in range(fields):
                            outs[kk][f] = outs[kk][f] + anoms[f] * w
                for kk in range(K):
                    for f, a in enumerate(lanes):
                        outgoing[dest * K + kk, i, :, a : a + band] = outs[kk][f]
        away = lax.rem(dest - m + M, M)
        target = out_ref.at[:, :, pl.ds(pl.multiple_of(m * C, C), C), :]

        @pl.when(away != 0)
        def _():
            pltpu.make_async_remote_copy(
                src_ref=outgoing.at[dest * K : (dest + 1) * K], dst_ref=target,
                send_sem=out_send.at[away], recv_sem=out_recv.at[away],
                device_id=(dest, g), device_id_type=MESH,
            ).start()

        @pl.when(away == 0)
        def _():
            pltpu.make_async_copy(outgoing.at[dest * K : (dest + 1) * K], target, local_sem.at[2]).start()

    far = M // 2

    @pl.when(m < far)
    def _():
        for dest in list(range(far, M)) + list(range(far)):
            update(dest)

    @pl.when(m >= far)
    def _():
        for dest in range(M):
            update(dest)

    for copy in sends:
        copy.wait_send()
    for dm, dg, src, dst, n in plans:
        @pl.when(near[dm, dg])
        def _():
            pltpu.make_async_remote_copy(
                src_ref=src, dst_ref=dst, send_sem=halo_send.at[n], recv_sem=halo_recv.at[n],
                device_id=(m + dm, g + dg), device_id_type=MESH,
            ).wait_send()
    pltpu.make_async_copy(
        outgoing.at[pl.ds(m * K, K)], out_ref.at[:, :, pl.ds(pl.multiple_of(m * C, C), C), :], local_sem.at[2]
    ).wait()
    for off in range(1, M):
        to = lax.rem(m + off, M)
        came = lax.rem(m + M - off, M)
        pltpu.make_async_remote_copy(
            src_ref=outgoing.at[pl.ds(to * K, K)],
            dst_ref=out_ref.at[:, :, pl.ds(pl.multiple_of(came * C, C), C), :],
            send_sem=out_send.at[off], recv_sem=out_recv.at[off],
            device_id=(to, g), device_id_type=MESH,
        ).wait()


def local(M, G, ensemble, obs_value, obs_error, obs_index, obs_count):
    K, R, cols, V = ensemble.shape
    O = obs_value.shape[2]
    C = cols // M
    members = M * K
    J = up_to(members + 1, 8)
    QP = up_to(members * J, LANES)
    slots_all = R * C * O
    targets = 4 * C * (R + 2)
    width = up_to(4 * C * R, LANES)
    pack_rows = up_to(3 * R, 8)
    f32 = jnp.float32
    vmem = pltpu.VMEM
    edge_rows = 4 * (R + 2)
    dma = pltpu.SemaphoreType.DMA
    flat = lambda a: a.reshape(a.shape[0], -1)
    return pl.pallas_call(
        functools.partial(kernel, (M, G, K, R, C, V, O, J, QP)),
        out_shape=pltpu.VMEM(ensemble.shape, f32),
        in_specs=[pl.BlockSpec(memory_space=pl.ANY)] * 4
        + [pl.BlockSpec(memory_space=pltpu.SMEM)],
        out_specs=pl.BlockSpec(memory_space=vmem),
        scratch_shapes=[
            vmem((G * R, O), f32),
            vmem((G * R, O), f32),
            vmem((G * R, O), jnp.int32),
            vmem((members, R, C, V), f32),
            vmem((G * pack_rows, O), f32),
            vmem((C * pack_rows, O), f32),
            vmem((R, C, V), f32),
            vmem((R * J * C, O), f32),
            vmem((2 * R, C, O), f32),
            vmem((2 * targets, slots_all), jnp.bfloat16),
            vmem((QP, slots_all), jnp.bfloat16),
            vmem((QP, slots_all), jnp.bfloat16),
            vmem((targets, QP), f32),
            vmem((2, edge_rows, QP), f32),
            vmem((2, 4 * C, QP), f32),
            vmem((6, edge_rows, QP), f32),
            vmem((width, QP), f32),
            vmem((members, J, width), f32),
            vmem((members, J, width), f32),
            vmem((members, J, width), f32),
            vmem((2, J, width), f32),
            vmem((QP, width), f32),
            vmem((members, R, C, V), f32),
            dma((M,)), dma((M,)), dma((G,)), dma((G,)), dma((8,)), dma((8,)), dma((M,)), dma((M,)), dma((6,)),
        ],
        compiler_params=pltpu.CompilerParams(
            collective_id=0, has_side_effects=True, vmem_limit_bytes=56 * 1024 * 1024
        ),
    )(ensemble, flat(obs_value), flat(obs_error), flat(obs_index), obs_count.reshape(1, -1))


def solution(mesh):
    return jax.shard_map(
        functools.partial(local, mesh.shape["member"], mesh.shape["region"]),
        mesh=mesh,
        in_specs=(
            P("member", "region", None, None),
            P(None, ("member", "region"), None),
            P(None, ("member", "region"), None),
            P(None, ("member", "region"), None),
            P(None, ("member", "region")),
        ),
        out_specs=P("member", "region", None, None),
        check_vma=False,
    )
```

profile of v0, /device:TPU:33, one launch (start us, length us, event | category | flops | bytes accessed | tf_op | source)
XLA Modules:
  0.0 74.5 jit_solution(8843172215861516004)
XLA Ops:
  0.0 73.3 %shard_map.55 = f32[3,2,128,512]{3,2,1,0:T(8,128)S(1)} custom-call(f32[3,2,128,512]{3,2,1,0:T(8,128)} %ens_ref.1, f32[32,128]{1,0:T(8,128)} %bitcast.4, f32[32,128]{1,0:T(8,128)} %bitcast.5, s32[32,128]{1,0:T(8,128)} %bitcast.6, s32[1,32]{1,0:T(1,128)} %bitcast.7), custom_call_target="tpu_custom_call" | custom-call | tf_op jit(solution)/shard_map/pallas_call | solution.py:437
  73.3 1.1 %copy.7 = f32[3,2,128,512]{3,2,1,0:T(8,128)} copy(f32[3,2,128,512]{3,2,1,0:T(8,128)S(1)} %shard_map.55) | data formatting | bytes 3145728
where the time goes:
time: 74.8 us; the launch traced here: 74.5 us
  Pallas kernels  73.3 us (98%)
  local copies, waits for them, and re-layouts  1.15 us (2%)
    pallas_call x1, Pallas kernels, local(): pl.pallas_call(functools.partial(kernel, (M, G, K, R, C, V, O, J, QP)), o...  73.3 us

commit v1 on v0

v1 whole, which is shorter than its diff:
```python
import functools
import math

import jax
import jax.numpy as jnp
from jax import lax
from jax.experimental import pallas as pl
from jax.experimental.pallas import tpu as pltpu
from jax.sharding import PartitionSpec as P

SIDE = 16
CELLS = SIDE * SIDE
HALF = SIDE // 2
LANES = 128
SUB = 8
NS_ITERS = 6
LOC_SCALE = 12.0
INFLATION_FACTOR = 1.1
MESH = pl.DeviceIdType.MESH
NT = (((1,), (1,)), ((), ()))
T = 8
PHASES = 2
OWN = 128
ROW_HALO = 32
SIDE_HALO = 16
TARGETS = 256


def split(values):
    high = values.astype(jnp.bfloat16)
    low = (values - high.astype(jnp.float32)).astype(jnp.bfloat16)
    return high, low


def row_of(k, jb):
    kb = k // SUB
    return (0, 192, 320)[kb] + (k - SUB * kb) * (24 - SUB * kb) + SUB * (jb - kb)


def kernel(
    dims,
    ens_ref, value_any, error_any, index_any, count_ref, out_ref,
    value_ref, error_ref, index_ref, ens, pack, obs, slots, place, lochi, loclo, qhi, qlo, own, hin,
    halo_out, row_in, side_in, root, inv, step, drv, half_ref, wt, xt, mean, outgoing,
    ens_send, ens_recv, obs_send, obs_recv, halo_send, halo_recv, out_send, out_recv, local_sem, own_sem,
):
    M, G, K, R, V, O = dims
    members = M * K
    blocks = members // SUB
    PACKED = own.shape[0]
    m = lax.axis_index("member")
    g = lax.axis_index("region")
    f32 = jnp.float32

    loads = []
    for n, (src, dst) in enumerate(((value_any, value_ref), (error_any, error_ref), (index_any, index_ref))):
        load = pltpu.make_async_copy(src, dst, local_sem.at[n])
        load.start()
        loads.append(load)

    def tile(p, d):
        return pl.ds(pl.multiple_of((p * M + d) * T, T), T)

    def own_copy(p):
        return pltpu.make_async_copy(
            ens_ref.at[:, :, tile(p, m), :], ens.at[p, pl.ds(m * K, K)], own_sem.at[p]
        )

    for p in range(PHASES):
        own_copy(p).start()

    column = m * G + g
    col_tile = column // T
    col_owner = lax.rem(col_tile, M)
    col_phase = col_tile // M
    col_at = lax.rem(column, T)
    holders = []
    for s in range(PHASES * T):
        c = ((s // T) * M + m) * T + s % T
        holders.append((c // G, lax.rem(c, G)))

    barrier = pltpu.get_barrier_semaphore()
    for off in range(1, M):
        pl.semaphore_signal(barrier, inc=1, device_id=(lax.rem(m + off, M), g), device_id_type=MESH)
    for hm, hg in holders:
        @pl.when(jnp.logical_not(jnp.logical_and(hm == m, hg == g)))
        def _():
            pl.semaphore_signal(barrier, inc=1, device_id=(hm, hg), device_id_type=MESH)
    up_ok = g > 0
    down_ok = g < G - 1
    row_ok = {-1: up_ok, 1: down_ok}
    for dg in (-1, 1):
        for dm in (-1, 0, 1):
            @pl.when(row_ok[dg])
            def _():
                pl.semaphore_signal(barrier, inc=1, device_id=(lax.rem(m + M + dm, M), g + dg), device_id_type=MESH)

    for load in loads:
        load.wait()
    slot = lax.broadcasted_iota(jnp.int32, (G * R, O), 1)
    slot_row = lax.broadcasted_iota(jnp.int32, (G * R, O), 0)
    count = jnp.zeros((G * R, O), jnp.int32)
    for d in range(G * R):
        count = jnp.where(slot_row == d, count_ref[0, d], count)
    live = jnp.where(slot < count, 1.0, 0.0).astype(f32)
    weight = jnp.sqrt(live / error_ref[...])
    value = value_ref[...]
    index_f = index_ref[...].astype(f32)
    for d in range(G):
        base = d * SUB
        pack[base : base + R, :] = weight[d * R : (d + 1) * R]
        pack[base + R : base + 2 * R, :] = value[d * R : (d + 1) * R]
        pack[base + 2 * R : base + 3 * R, :] = index_f[d * R : (d + 1) * R]
        pack[base + 3 * R : base + SUB, :] = jnp.zeros((SUB - 3 * R, O), f32)
    used = OWN + 2 * ROW_HALO
    lochi[used:, :] = jnp.zeros((TARGETS - used, lochi.shape[1]), jnp.bfloat16)
    loclo[used:, :] = jnp.zeros((TARGETS - used, lochi.shape[1]), jnp.bfloat16)

    ends = jnp.where(up_ok, 1, 0) + jnp.where(down_ok, 1, 0)
    self_obs = jnp.where(col_owner == m, 1, 0)
    pl.semaphore_wait(barrier, M - 1 + G - self_obs + 3 * ends)

    pieces = ((0, 1), (1, K))

    def ens_copy(p, n, off, to, at):
        a, b = pieces[n]
        return pltpu.make_async_remote_copy(
            src_ref=ens_ref.at[a:b, :, tile(p, to), :],
            dst_ref=ens.at[p, pl.ds(at * K + a, b - a)],
            send_sem=ens_send.at[p, n, off], recv_sem=ens_recv.at[p, n, off],
            device_id=(to, g), device_id_type=MESH,
        )

    def obs_copy(to_m, to_g, src_g, p, e):
        return pltpu.make_async_remote_copy(
            src_ref=pack.at[pl.ds(pl.multiple_of(src_g * SUB, SUB), SUB)],
            dst_ref=obs.at[p, pl.ds(pl.multiple_of(e * SUB, SUB), SUB)],
            send_sem=obs_send.at[src_g], recv_sem=obs_recv.at[p, e],
            device_id=(to_m, to_g), device_id_type=MESH,
        )

    for off in range(1, G):
        to = lax.rem(g + off, G)
        obs_copy(col_owner, to, to, col_phase, col_at).start()

    @pl.when(col_owner != m)
    def _():
        obs_copy(col_owner, g, g, col_phase, col_at).start()

    @pl.when(col_owner == m)
    def _():
        obs[col_phase, pl.ds(pl.multiple_of(col_at * SUB, SUB), SUB), :] = pack[
            pl.ds(pl.multiple_of(g * SUB, SUB), SUB), :
        ]

    order = [4, 5, 3, 2, 6, 1, 7]
    order = [off for off in order if off < M] + [off for off in range(1, M) if off not in order]
    for n in range(2):
        for off in order:
            ens_copy(0, n, off, lax.rem(m + off, M), m).start()
    for off in order:
        ens_copy(1, 0, off, lax.rem(m + off, M), m).start()
    for off in order:
        to = lax.rem(m + off, M)
        @pl.when(to == 0)
        def _():
            ens_copy(1, 1, off, to, m).start()

    for s, (hm, hg) in enumerate(holders):
        @pl.when(jnp.logical_not(jnp.logical_and(hm == m, hg == g)))
        def _():
            obs_copy(hm, hg, g, s // T, s % T).wait_recv()

    def wait_ens(p):
        own_copy(p).wait()
        for n in range(2):
            for off in range(1, M):
                came = lax.rem(m + M - off, M)
                ens_copy(p, n, off, came, came).wait_recv()

    tiles = V // LANES

    def gather(p):
        for i in range(R):
            wgt = obs[p, pl.ds(i, T, stride=SUB), :]
            val = obs[p, pl.ds(R + i, T, stride=SUB), :]
            idx = obs[p, pl.ds(2 * R + i, T, stride=SUB), :].astype(jnp.int32)
            lane = idx & (LANES - 1)
            which = idx >> 7
            cell = idx & (CELLS - 1)
            place[2 * i] = (cell >> 4).astype(f32)
            place[2 * i + 1] = (cell & (SIDE - 1)).astype(f32)
            seen = []
            for k in range(members):
                got = jnp.take_along_axis(ens[p, k, i, :, :LANES], lane, axis=1)
                for t in range(1, tiles):
                    more = jnp.take_along_axis(ens[p, k, i, :, t * LANES : (t + 1) * LANES], lane, axis=1)
                    got = jnp.where(which == t, more, got)
                seen.append(got)
            total = seen[0]
            for k in range(1, members):
                total = total + seen[k]
            avg = total * (1.0 / members)
            for k in range(members):
                slots[i, k * T : (k + 1) * T, :] = wgt * (seen[k] - avg)
            slots[i, members * T : (members + 1) * T, :] = wgt * (val - avg)

    sub8 = lax.broadcasted_iota(jnp.int32, (SUB, O), 0)

    def products(c, i):
        at = (c * R + i) * O
        here = [slots[i, pl.ds(c + b * SUB * T, SUB, stride=T), :] for b in range(blocks)]
        innov = slots[i, members * T + c : members * T + c + 1, :]
        rows = []
        for k in range(members):
            kb = k // SUB
            left = here[kb][k % SUB : k % SUB + 1]
            for jb in range(kb, blocks):
                right = here[jb]
                use = left
                if jb == kb and k % SUB == SUB - 1:
                    use = jnp.where(sub8 < SUB - 1, innov, left)
                if jb == kb and k % SUB == SUB - 2:
                    use = jnp.where(sub8 < 1, innov, left)
                    right = jnp.where(sub8 < 1, right[SUB - 1 : SUB], right)
                rows.append(use * right)
        for n in range(0, len(rows), 2):
            high, low = split(jnp.concatenate(rows[n : n + 2], axis=0))
            qhi[n * SUB : (n + 2) * SUB, at : at + O] = high
            qlo[n * SUB : (n + 2) * SUB, at : at + O] = low

    scale = -1.0 / (2.0 * LOC_SCALE * LOC_SCALE)
    middle = (HALF - 1) * 0.5
    t_id = lax.broadcasted_iota(jnp.int32, (SUB, O), 0)
    t_row = t_id >> 1
    t_mid = (t_id & 1).astype(f32) * HALF + middle
    col = lax.broadcasted_iota(jnp.int32, (T, O), 0)

    def row_weight(c, i):
        y = place[2 * i, c : c + 1, :]
        row_off = i + 1 - t_row
        dy = (row_off * SIDE).astype(f32) + y - t_mid
        return jnp.where(jnp.abs(row_off) <= 1, jnp.exp(dy * dy * scale), 0.0)

    def edge_weight(c, i, ly, away):
        x = place[2 * i + 1, c : c + 1, :]
        parts = []
        for pc in range(2):
            dx = away * SIDE + x - (pc * HALF + middle)
            parts.append(ly * jnp.exp(dx * dx * scale))
        return jnp.concatenate(parts, axis=0)

    def locality(c, i):
        at = (c * R + i) * O
        x = place[2 * i + 1, c : c + 1, :]
        ly = row_weight(c, i)
        col_off = c - col
        lx = []
        for pc in range(2):
            dx = (col_off * SIDE).astype(f32) + x - (pc * HALF + middle)
            lx.append(jnp.where(jnp.abs(col_off) <= 1, jnp.exp(dx * dx * scale), 0.0))

        def put(first, values):
            high, low = split(values)
            for at_row in first:
                lochi[at_row : at_row + values.shape[0], at : at + O] = high
                loclo[at_row : at_row + values.shape[0], at : at + O] = low

        for pc in range(2):
            for it in range(R):
                s = 2 * (it + 1)
                pair = jnp.concatenate([ly[s : s + 1] * lx[pc], ly[s + 1 : s + 2] * lx[pc]], axis=0)
                first = (pc * R + it) * 2 * T
                put((first, OWN // 2 + first), pair)
            for n, s in enumerate((0, 2 * (R + 1))):
                pair = jnp.concatenate([ly[s : s + 1] * lx[pc], ly[s + 1 : s + 2] * lx[pc]], axis=0)
                put((OWN + n * ROW_HALO + pc * 2 * T,), pair)
        if c == 0:
            put((used,), edge_weight(c, i, ly, 1))
        if c == T - 1:
            put((used + SIDE_HALO,), edge_weight(c, i, ly, -1))

    def dot(left, right):
        return lax.dot_general(left, right, NT, preferred_element_type=f32)

    def halo_plan(p, dm, dg):
        n = (dm + 1) * 3 + dg + 1
        send = row_ok[dg] if dg else jnp.bool_(True)
        recv = row_ok[-dg] if dg else jnp.bool_(True)
        at = p
        if dm == 0:
            first = 0 if dg < 0 else ROW_HALO
            src = halo_out.at[p, pl.ds(first, ROW_HALO)]
            dst = row_in.at[p, 0 if dg < 0 else 1]
            come = p
        else:
            if dm < 0:
                send = jnp.logical_and(send, jnp.logical_or(m > 0, p == 0))
                recv = jnp.logical_and(recv, jnp.logical_or(m < M - 1, p == 0))
            else:
                send = jnp.logical_and(send, jnp.logical_or(m < M - 1, p == 0))
                recv = jnp.logical_and(recv, jnp.logical_or(m > 0, p == 1))
                at = jnp.where(m == M - 1, 1, p)
            first = 2 * ROW_HALO + (0 if dm < 0 else SIDE_HALO)
            src = halo_out.at[p, pl.ds(first, SIDE_HALO)]
            base = (0 if dm < 0 else 3) + dg + 1
            dst = side_in.at[at, base]
            come = p

        def copy(slot, to_m, to_g):
            target = row_in.at[slot, 0 if dg < 0 else 1] if dm == 0 else side_in.at[slot, (0 if dm < 0 else 3) + dg + 1]
            return pltpu.make_async_remote_copy(
                src_ref=src, dst_ref=target, send_sem=halo_send.at[p, n], recv_sem=halo_recv.at[slot, n],
                device_id=(to_m, to_g), device_id_type=MESH,
            )

        outward = lambda: copy(at, lax.rem(m + M + dm, M), g + dg)
        inward = lambda: copy(p, lax.rem(m + M - dm, M), g - dg)
        landing = row_in.at[p, 0 if dg < 0 else 1] if dm == 0 else side_in.at[p, (0 if dm < 0 else 3) + dg + 1]
        return send, recv, outward, inward, landing

    near = [(dm, dg) for dm in (0, 1, -1) for dg in (-1, 0, 1) if (dm, dg) != (0, 0)]
    lane = lax.broadcasted_iota(jnp.int32, (SUB, OWN), 1)
    west = (lane & 32) == 0
    sub = lax.broadcasted_iota(jnp.int32, (SUB, OWN), 0)

    def square(left, right, into, first):
        for kb in range(blocks):
            for k0 in range(kb * SUB, (kb + 1) * SUB, 4):
                ks = range(k0, k0 + 4)
                sums = {}
                for i in range(members):
                    rights = [right[i * members + SUB * jb : i * members + SUB * (jb + 1), :] for jb in range(kb, blocks)]
                    for k in ks:
                        lone = left[k * members + i : k * members + i + 1, :]
                        for jb in range(kb, blocks):
                            term = lone * rights[jb - kb]
                            sums[k, jb] = term if i == 0 else sums[k, jb] + term
                for k in ks:
                    for jb in range(kb, blocks):
                        out = sums[k, jb]
                        if first:
                            out = -0.5 * out
                            if jb == kb:
                                out = out + jnp.where(sub == k % SUB, 1.5, 0.0)
                        put_entry(into, k, jb, out)

    def put_entry(into, k, jb, out):
        into[k * members + SUB * jb : k * members + SUB * (jb + 1), :] = out
        if jb > k // SUB:
            into[pl.ds(SUB * jb * members + k, SUB, stride=members), :] = out

    fields = V // CELLS
    halves = CELLS // LANES

    def phase(p, carry):
        first_phase = p == 0

        @pl.when(jnp.logical_or(first_phase, m > 0))
        def _():
            wait_ens(p)

        gather(p)
        for c in range(T):
            for i in range(R):
                products(c, i)
                locality(c, i)
        both = dot(qhi[...], lochi[...]) + dot(qhi[...], loclo[...]) + dot(qlo[...], lochi[...])
        own[...] = both[:, :OWN]
        halo_out[p] = jnp.transpose(both[:, OWN:])[: halo_out.shape[1]]

        plans = [halo_plan(p, dm, dg) for dm, dg in near]
        for (dm, dg), (send, recv, outward, inward, landing) in zip(near, plans):
            if dm >= 0:
                @pl.when(send)
                def _():
                    outward().start()

        @pl.when(jnp.logical_and(first_phase, m == 0))
        def _():
            wait_ens(1)
            gather(1)
            edges = []
            for i in range(R):
                products(0, i)
                edges.append(edge_weight(0, i, row_weight(0, i), 1))
            high, low = split(jnp.concatenate(edges, axis=1))
            seam = qhi[:, : R * O]
            halo_out[0, 2 * ROW_HALO : 2 * ROW_HALO + SIDE_HALO, :] = (
                dot(high, seam) + dot(low, seam) + dot(high, qlo[:, : R * O])
            )

        for (dm, dg), (send, recv, outward, inward, landing) in zip(near, plans):
            if dm < 0:
                @pl.when(send)
                def _():
                    outward().start()

        @pl.when(first_phase)
        def _():
            for off in order:
                to = lax.rem(m + off, M)
                @pl.when(to != 0)
                def _():
                    ens_copy(1, 1, off, to, m).start()

        total = None
        for k in range(members):
            rows = []
            for f in range(fields):
                part = [
                    ens[p, k, i, :, f * CELLS + h * LANES : f * CELLS + (h + 1) * LANES]
                    for i in range(R) for h in range(halves)
                ]
                rows += part + part
            turned = jnp.transpose(jnp.concatenate(rows, axis=0))
            lines = []
            for r in range(SUB):
                lines.append(jnp.where(west, turned[16 * r : 16 * r + 8], turned[16 * r + 8 : 16 * r + 16]))
            for r in range(SUB):
                xt[k, r * SUB : (r + 1) * SUB, :] = lines[r]
            total = lines if total is None else [a + b for a, b in zip(total, lines)]
        avg = [line * (1.0 / members) for line in total]
        for r in range(SUB):
            mean[r * SUB : (r + 1) * SUB, :] = avg[r]
        for k in range(members):
            for r in range(SUB):
                xt[k, r * SUB : (r + 1) * SUB, :] = xt[k, r * SUB : (r + 1) * SUB, :] - avg[r]

        for send, recv, outward, inward, landing in plans:
            @pl.when(recv)
            def _():
                inward().wait_recv()

            @pl.when(jnp.logical_not(recv))
            def _():
                landing[...] = jnp.zeros(landing.shape, f32)

        col8 = lax.broadcasted_iota(jnp.int32, (T, PACKED), 0)
        for pc in range(2):
            for i in range(R):
                for pr in range(2):
                    at = (pc * 2 + pr) * T
                    block = None
                    if i == R - 1:
                        block = row_in[p, 0, at : at + T, :]
                    if i == 0:
                        more = row_in[p, 1, at : at + T, :]
                        block = more if block is None else block + more
                    for base, at_col in ((0, T - 1), (3, 0)):
                        def pick(dg, t):
                            place_in = pc * SUB + t * 2 + pr
                            return side_in[p, base + dg + 1, place_in : place_in + 1, :]

                        line = pick(0, i + 1)
                        if i == R - 1:
                            line = line + pick(-1, 0)
                        if i == 0:
                            line = line + pick(1, R + 1)
                        more = jnp.where(col8 == at_col, line, 0.0)
                        block = more if block is None else block + more
                    at = ((pc * R + i) * 2 + pr) * T
                    hin[at : at + T, :] = block
                    hin[OWN // 2 + at : OWN // 2 + at + T, :] = block
        prec = own[...] + jnp.transpose(hin[...])

        for b in range(blocks):
            top = prec[row_of(SUB * b + SUB - 1, b) : row_of(SUB * b + SUB - 1, b) + SUB]
            last = prec[row_of(SUB * b + SUB - 2, b) : row_of(SUB * b + SUB - 2, b) + 1]
            drv[SUB * b : SUB * (b + 1), :] = jnp.where(sub < SUB - 1, top, last)
        y0, y1, z0, z1 = root.at[0], root.at[1], inv.at[0], inv.at[1]
        inflate = (members - 1) / INFLATION_FACTOR
        for k in range(members):
            kb = k // SUB
            for jb in range(kb, blocks):
                out = prec[row_of(k, jb) : row_of(k, jb) + SUB]
                if jb == kb:
                    keep = {SUB - 1: sub >= SUB - 1, SUB - 2: sub >= 1}.get(k % SUB)
                    if keep is not None:
                        out = jnp.where(keep, out, 0.0)
                    out = out + jnp.where(sub == k % SUB, inflate, 0.0)
                put_entry(y1, k, jb, out)
        for b in range(blocks):
            for e in (SUB - 1, SUB - 2):
                k = SUB * b + e
                y1[k * members + SUB * b : k * members + SUB * (b + 1), :] = y1[
                    pl.ds(SUB * b * members + k, SUB, stride=members), :
                ]
        squares = None
        for n in range(members * blocks):
            line = y1[n * SUB : (n + 1) * SUB, :]
            squares = line * line if squares is None else squares + line * line
        norm = jnp.sqrt(jnp.sum(squares, axis=0, keepdims=True))
        small = 1.0 / norm
        for k in range(members):
            for jb in range(blocks):
                rows = slice(k * members + SUB * jb, k * members + SUB * (jb + 1))
                start = y1[rows, :] * small
                first_m = -0.5 * start
                if jb == k // SUB:
                    first_m = first_m + jnp.where(sub == k % SUB, 1.5, 0.0)
                y1[rows, :] = start
                step[rows, :] = first_m
                z0[rows, :] = first_m
        square(y1, step, y0, False)

        def sweep(n, carry):
            now = lax.rem(n, 2)
            square(inv.at[now], root.at[now], step, True)
            square(root.at[now], step, root.at[1 - now], False)
            square(inv.at[now], step, inv.at[1 - now], False)
            return carry

        lax.fori_loop(0, NS_ITERS - 2, sweep, 0)
        square(z0, y0, step, True)
        square(z0, step, z1, False)

        shrink = 1.0 / jnp.sqrt(norm)

        def applied(vector):
            sums = [None] * blocks
            for i in range(members):
                lone = vector[i : i + 1, :]
                for jb in range(blocks):
                    term = lone * z1[i * members + SUB * jb : i * members + SUB * (jb + 1), :]
                    sums[jb] = term if i == 0 else sums[jb] + term
            return [line * shrink for line in sums]

        for jb, line in enumerate(applied(drv)):
            half_ref[SUB * jb : SUB * (jb + 1), :] = line
        mean_w = applied(half_ref)
        spread = math.sqrt(members - 1) * shrink
        for k in range(members):
            for jb in range(blocks):
                wt[k, SUB * jb : SUB * (jb + 1), :] = (
                    mean_w[jb] + spread * z1[k * members + SUB * jb : k * members + SUB * (jb + 1), :]
                )

        chips = M // 2
        group = 2 * K

        def update(q, carry):
            away_chip = jnp.where(q == 0, chips // 2, jnp.where(q == chips - 1, 0, jnp.where(q == 1, 1, chips - 1)))
            chip = lax.rem(m // 2 + away_chip, chips)
            k0 = chip * group
            for pair in range(0, group, 2):
                sums = [[mean[r * SUB : (r + 1) * SUB, :] for r in range(SUB)] for _ in range(2)]
                for j in range(members):
                    lines = [xt[j, r * SUB : (r + 1) * SUB, :] for r in range(SUB)]
                    for e in range(2):
                        lone = wt[k0 + pair + e, j : j + 1, :]
                        sums[e] = [s + lone * line for s, line in zip(sums[e], lines)]
                rows = []
                for r in range(SUB):
                    one, two = sums[0][r], sums[1][r]
                    rows.append(jnp.where(west, one, pltpu.roll(two, 32, 1)))
                    rows.append(jnp.where(west, pltpu.roll(one, OWN - 32, 1), two))
                turned = jnp.transpose(jnp.concatenate(rows, axis=0))
                at = 0
                for f in range(fields):
                    for e in range(2):
                        for i in range(R):
                            for h in range(halves):
                                lanes = f * CELLS + h * LANES
                                outgoing[p, k0 + pair + e, i, :, lanes : lanes + LANES] = turned[at : at + T]
                                at += T
            for core in range(2):
                dest = 2 * chip + core
                away = lax.rem(dest - m + M, M)

                @pl.when(away != 0)
                def _():
                    out_copy(p, away, dest, m).start()

                @pl.when(away == 0)
                def _():
                    out_ref[:, :, tile(p, m), :] = outgoing[p, pl.ds(dest * K, K)]
            return carry

        lax.fori_loop(0, chips, update, 0)
        return carry

    def out_copy(p, away, dest, source):
        return pltpu.make_async_remote_copy(
            src_ref=outgoing.at[p, pl.ds(dest * K, K)],
            dst_ref=out_ref.at[:, :, tile(p, source), :],
            send_sem=out_send.at[p, away], recv_sem=out_recv.at[p, away],
            device_id=(dest, g), device_id_type=MESH,
        )

    lax.fori_loop(0, PHASES, phase, 0)

    for off in range(1, G):
        to = lax.rem(g + off, G)
        obs_copy(col_owner, to, to, col_phase, col_at).wait_send()

    @pl.when(col_owner != m)
    def _():
        obs_copy(col_owner, g, g, col_phase, col_at).wait_send()

    for p in range(PHASES):
        for n in range(2):
            for off in range(1, M):
                ens_copy(p, n, off, lax.rem(m + off, M), m).wait_send()
        for dm, dg in near:
            send, recv, outward, inward, landing = halo_plan(p, dm, dg)

            @pl.when(send)
            def _():
                outward().wait_send()
    for p in range(PHASES):
        for off in range(1, M):
            out_copy(p, off, lax.rem(m + off, M), m).wait_send()
            out_copy(p, off, m, lax.rem(m + M - off, M)).wait_recv()


def local(M, G, ensemble, obs_value, obs_error, obs_index, obs_count):
    K, R, cols, V = ensemble.shape
    O = obs_value.shape[2]
    members = M * K
    assert cols == PHASES * M * T and cols == M * G and R == 2 and members == 24 and V == 2 * CELLS and O == LANES
    wide = T * R * O
    packed = 384
    square = members * members
    f32 = jnp.float32
    vmem = pltpu.VMEM
    dma = pltpu.SemaphoreType.DMA
    flat = lambda a: a.reshape(a.shape[0], -1)
    return pl.pallas_call(
        functools.partial(kernel, (M, G, K, R, V, O)),
        out_shape=pltpu.VMEM(ensemble.shape, f32),
        in_specs=[pl.BlockSpec(memory_space=pl.ANY)] * 4
        + [pl.BlockSpec(memory_space=pltpu.SMEM)],
        out_specs=pl.BlockSpec(memory_space=vmem),
        scratch_shapes=[
            vmem((G * R, O), f32),
            vmem((G * R, O), f32),
            vmem((G * R, O), jnp.int32),
            vmem((PHASES, members, R, T, V), f32),
            vmem((G * SUB, O), f32),
            vmem((PHASES, T * SUB, O), f32),
            vmem((R, (members + 1) * T, O), f32),
            vmem((2 * R, T, O), f32),
            vmem((TARGETS, wide), jnp.bfloat16),
            vmem((TARGETS, wide), jnp.bfloat16),
            vmem((packed, wide), jnp.bfloat16),
            vmem((packed, wide), jnp.bfloat16),
            vmem((packed, OWN), f32),
            vmem((OWN, packed), f32),
            vmem((PHASES, 2 * ROW_HALO + 2 * SIDE_HALO, packed), f32),
            vmem((PHASES, 2, ROW_HALO, packed), f32),
            vmem((PHASES, 6, SIDE_HALO, packed), f32),
            vmem((2, square, OWN), f32),
            vmem((2, square, OWN), f32),
            vmem((square, OWN), f32),
            vmem((members, OWN), f32),
            vmem((members, OWN), f32),
            vmem((members, members, OWN), f32),
            vmem((members, SUB * SUB, OWN), f32),
            vmem((SUB * SUB, OWN), f32),
            vmem((PHASES, members, R, T, V), f32),
            dma((PHASES, 2, M)), dma((PHASES, 2, M)), dma((G,)), dma((PHASES, T)),
            dma((PHASES, 9)), dma((PHASES, 9)), dma((PHASES, M)), dma((PHASES, M)), dma((3,)), dma((PHASES,)),
        ],
        compiler_params=pltpu.CompilerParams(
            collective_id=0, has_side_effects=True, vmem_limit_bytes=56 * 1024 * 1024
        ),
    )(ensemble, flat(obs_value), flat(obs_error), flat(obs_index), obs_count.reshape(1, -1))


def solution(mesh):
    return jax.shard_map(
        functools.partial(local, mesh.shape["member"], mesh.shape["region"]),
        mesh=mesh,
        in_specs=(
            P("member", "region", None, None),
            P(None, ("member", "region"), None),
            P(None, ("member", "region"), None),
            P(None, ("member", "region"), None),
            P(None, ("member", "region")),
        ),
        out_specs=P("member", "region", None, None),
        check_vma=False,
    )
```

time: 74.8 us -> 64.9 us (0.87)
  Pallas kernels: 73.3 us -> 63.6 us
    pallas_call x1, Pallas kernels: 73.3 us -> 63.6 us  [local(): pl.pallas_call(functools.partial(kernel, (M, G, K, R, V, O)), out_shape=p...]
where the time goes in v1:
time: 64.9 us; the launch traced here: 64.8 us
  Pallas kernels  63.6 us (98%)
  local copies, waits for them, and re-layouts  1.15 us (2%)
    pallas_call x1, Pallas kernels, local(): pl.pallas_call(functools.partial(kernel, (M, G, K, R, V, O)), out_shape=p...  63.6 us

profile of v1, /device:TPU:33, one launch (start us, length us, event | category | flops | bytes accessed | tf_op | source)
XLA Modules:
  0.0 64.8 jit_solution(13717400496219347342)
XLA Ops:
  0.0 63.6 %shard_map.55 = f32[3,2,128,512]{3,2,1,0:T(8,128)S(1)} custom-call(f32[3,2,128,512]{3,2,1,0:T(8,128)} %ens_ref.1, f32[32,128]{1,0:T(8,128)} %bitcast.4, f32[32,128]{1,0:T(8,128)} %bitcast.5, s32[32,128]{1,0:T(8,128)} %bitcast.6, s32[1,32]{1,0:T(1,128)} %bitcast.7), custom_call_target="tpu_custom_call" | custom-call | tf_op jit(solution)/shard_map/pallas_call | solution.py:629
  63.6 1.1 %copy.7 = f32[3,2,128,512]{3,2,1,0:T(8,128)} copy(f32[3,2,128,512]{3,2,1,0:T(8,128)S(1)} %shard_map.55) | data formatting | bytes 3145728

commit v2 on v1

--- a/solution.py
+++ b/solution.py
@@ -42,7 +42,7 @@
     ens_ref, value_any, error_any, index_any, count_ref, out_ref,
     value_ref, error_ref, index_ref, ens, pack, obs, slots, place, lochi, loclo, qhi, qlo, own, hin,
     halo_out, row_in, side_in, root, inv, step, drv, half_ref, wt, xt, mean, outgoing,
-    ens_send, ens_recv, obs_send, obs_recv, halo_send, halo_recv, out_send, out_recv, local_sem, own_sem,
+    ens_send, ens_recv, obs_send, obs_recv, halo_send, halo_recv, out_send, out_recv, local_sem, own_sem, entry_sem,
 ):
     M, G, K, R, V, O = dims
     members = M * K
@@ -79,21 +79,47 @@
         c = ((s // T) * M + m) * T + s % T
         holders.append((c // G, lax.rem(c, G)))
 
+    ring = 4
+    y, z = lax.rem(g, ring), g // ring
+    x_peers = [(lax.rem(m + off, M), g) for off in range(1, M)]
+    y_peers = [(m, z * ring + lax.rem(y + off, ring)) for off in range(1, ring)]
+    z_peers = [(m, lax.rem(g + off * ring, G)) for off in range(1, G // ring)]
     barrier = pltpu.get_barrier_semaphore()
-    for off in range(1, M):
-        pl.semaphore_signal(barrier, inc=1, device_id=(lax.rem(m + off, M), g), device_id_type=MESH)
-    for hm, hg in holders:
-        @pl.when(jnp.logical_not(jnp.logical_and(hm == m, hg == g)))
-        def _():
-            pl.semaphore_signal(barrier, inc=1, device_id=(hm, hg), device_id_type=MESH)
+    for peer in x_peers + y_peers + z_peers:
+        pl.semaphore_signal(barrier, inc=1, device_id=peer, device_id_type=MESH)
     up_ok = g > 0
     down_ok = g < G - 1
     row_ok = {-1: up_ok, 1: down_ok}
-    for dg in (-1, 1):
-        for dm in (-1, 0, 1):
-            @pl.when(row_ok[dg])
-            def _():
-                pl.semaphore_signal(barrier, inc=1, device_id=(lax.rem(m + M + dm, M), g + dg), device_id_type=MESH)
+    pl.semaphore_wait(barrier, len(x_peers) + len(y_peers) + len(z_peers))
+    for peer in y_peers:
+        pl.semaphore_signal(entry_sem.at[0], inc=1, device_id=peer, device_id_type=MESH)
+
+    pieces = ((0, 1), (1, K))
+
+    def ens_copy(p, n, off, to, at):
+        a, b = pieces[n]
+        return pltpu.make_async_remote_copy(
+            src_ref=ens_ref.at[a:b, :, tile(p, to), :],
+            dst_ref=ens.at[p, pl.ds(at * K + a, b - a)],
+            send_sem=ens_send.at[p, n, off], recv_sem=ens_recv.at[p, n, off],
+            device_id=(to, g), device_id_type=MESH,
+        )
+
+    order = [4, 5, 3, 2, 6, 1, 7]
+    order = [off for off in order if off < M] + [off for off in range(1, M) if off not in order]
+    for n in range(2):
+        for off in order:
+            ens_copy(0, n, off, lax.rem(m + off, M), m).start()
+    pl.semaphore_wait(entry_sem.at[0], len(y_peers))
+    for peer in x_peers:
+        pl.semaphore_signal(entry_sem.at[1], inc=1, device_id=peer, device_id_type=MESH)
+    for off in order:
+        ens_copy(1, 0, off, lax.rem(m + off, M), m).start()
+    for off in order:
+        to = lax.rem(m + off, M)
+        @pl.when(to == 0)
+        def _():
+            ens_copy(1, 1, off, to, m).start()
 
     for load in loads:
         load.wait()
@@ -116,20 +142,7 @@
     lochi[used:, :] = jnp.zeros((TARGETS - used, lochi.shape[1]), jnp.bfloat16)
     loclo[used:, :] = jnp.zeros((TARGETS - used, lochi.shape[1]), jnp.bfloat16)
 
-    ends = jnp.where(up_ok, 1, 0) + jnp.where(down_ok, 1, 0)
-    self_obs = jnp.where(col_owner == m, 1, 0)
-    pl.semaphore_wait(barrier, M - 1 + G - self_obs + 3 * ends)
-
-    pieces = ((0, 1), (1, K))
-
-    def ens_copy(p, n, off, to, at):
-        a, b = pieces[n]
-        return pltpu.make_async_remote_copy(
-            src_ref=ens_ref.at[a:b, :, tile(p, to), :],
-            dst_ref=ens.at[p, pl.ds(at * K + a, b - a)],
-            send_sem=ens_send.at[p, n, off], recv_sem=ens_recv.at[p, n, off],
-            device_id=(to, g), device_id_type=MESH,
-        )
+    pl.semaphore_wait(entry_sem.at[1], len(x_peers))
 
     def obs_copy(to_m, to_g, src_g, p, e):
         return pltpu.make_async_remote_copy(
@@ -152,19 +165,6 @@
         obs[col_phase, pl.ds(pl.multiple_of(col_at * SUB, SUB), SUB), :] = pack[
             pl.ds(pl.multiple_of(g * SUB, SUB), SUB), :
         ]
-
-    order = [4, 5, 3, 2, 6, 1, 7]
-    order = [off for off in order if off < M] + [off for off in range(1, M) if off not in order]
-    for n in range(2):
-        for off in order:
-            ens_copy(0, n, off, lax.rem(m + off, M), m).start()
-    for off in order:
-        ens_copy(1, 0, off, lax.rem(m + off, M), m).start()
-    for off in order:
-        to = lax.rem(m + off, M)
-        @pl.when(to == 0)
-        def _():
-            ens_copy(1, 1, off, to, m).start()
 
     for s, (hm, hg) in enumerate(holders):
         @pl.when(jnp.logical_not(jnp.logical_and(hm == m, hg == g)))
@@ -353,6 +353,50 @@
     fields = V // CELLS
     halves = CELLS // LANES
 
+    def results(p):
+        chips = M // 2
+        group = 2 * K
+
+        def update(q, carry):
+            away_chip = jnp.where(q == 0, chips // 2, jnp.where(q == chips - 1, 0, jnp.where(q == 1, 1, chips - 1)))
+            chip = lax.rem(m // 2 + away_chip, chips)
+            k0 = chip * group
+            for pair in range(0, group, 2):
+                sums = [[mean[r * SUB : (r + 1) * SUB, :] for r in range(SUB)] for _ in range(2)]
+                for j in range(members):
+                    lines = [xt[j, r * SUB : (r + 1) * SUB, :] for r in range(SUB)]
+                    for e in range(2):
+                        lone = wt[k0 + pair + e, j : j + 1, :]
+                        sums[e] = [s + lone * line for s, line in zip(sums[e], lines)]
+                rows = []
+                for r in range(SUB):
+                    one, two = sums[0][r], sums[1][r]
+                    rows.append(jnp.where(west, one, pltpu.roll(two, 32, 1)))
+                    rows.append(jnp.where(west, pltpu.roll(one, OWN - 32, 1), two))
+                turned = jnp.transpose(jnp.concatenate(rows, axis=0))
+                at = 0
+                for f in range(fields):
+                    for e in range(2):
+                        for i in range(R):
+                            for h in range(halves):
+                                lanes = f * CELLS + h * LANES
+                                outgoing[p, k0 + pair + e, i, :, lanes : lanes + LANES] = turned[at : at + T]
+                                at += T
+            for core in range(2):
+                dest = 2 * chip + core
+                away = lax.rem(dest - m + M, M)
+
+                @pl.when(away != 0)
+                def _():
+                    out_copy(p, away, dest, m).start()
+
+                @pl.when(away == 0)
+                def _():
+                    out_ref[:, :, tile(p, m), :] = outgoing[p, pl.ds(dest * K, K)]
+            return carry
+
+        lax.fori_loop(0, chips, update, 0)
+
     def phase(p, carry):
         first_phase = p == 0
 
@@ -403,6 +447,10 @@
                 @pl.when(to != 0)
                 def _():
                     ens_copy(1, 1, off, to, m).start()
+
+        @pl.when(p > 0)
+        def _():
+            results(p - 1)
 
         total = None
         for k in range(members):
@@ -536,48 +584,6 @@
                     mean_w[jb] + spread * z1[k * members + SUB * jb : k * members + SUB * (jb + 1), :]
                 )
 
-        chips = M // 2
-        group = 2 * K
-
-        def update(q, carry):
-            away_chip = jnp.where(q == 0, chips // 2, jnp.where(q == chips - 1, 0, jnp.where(q == 1, 1, chips - 1)))
-            chip = lax.rem(m // 2 + away_chip, chips)
-            k0 = chip * group
-            for pair in range(0, group, 2):
-                sums = [[mean[r * SUB : (r + 1) * SUB, :] for r in range(SUB)] for _ in range(2)]
-                for j in range(members):
-                    lines = [xt[j, r * SUB : (r + 1) * SUB, :] for r in range(SUB)]
-                    for e in range(2):
-                        lone = wt[k0 + pair + e, j : j + 1, :]
-                        sums[e] = [s + lone * line for s, line in zip(sums[e], lines)]
-                rows = []
-                for r in range(SUB):
-                    one, two = sums[0][r], sums[1][r]
-                    rows.append(jnp.where(west, one, pltpu.roll(two, 32, 1)))
-                    rows.append(jnp.where(west, pltpu.roll(one, OWN - 32, 1), two))
-                turned = jnp.transpose(jnp.concatenate(rows, axis=0))
-                at = 0
-                for f in range(fields):
-                    for e in range(2):
-                        for i in range(R):
-                            for h in range(halves):
-                                lanes = f * CELLS + h * LANES
-                                outgoing[p, k0 + pair + e, i, :, lanes : lanes + LANES] = turned[at : at + T]
-                                at += T
-            for core in range(2):
-                dest = 2 * chip + core
-                away = lax.rem(dest - m + M, M)
-
-                @pl.when(away != 0)
-                def _():
-                    out_copy(p, away, dest, m).start()
-
-                @pl.when(away == 0)
-                def _():
-                    out_ref[:, :, tile(p, m), :] = outgoing[p, pl.ds(dest * K, K)]
-            return carry
-
-        lax.fori_loop(0, chips, update, 0)
         return carry
 
     def out_copy(p, away, dest, source):
@@ -589,6 +595,7 @@
         )
 
     lax.fori_loop(0, PHASES, phase, 0)
+    results(PHASES - 1)
 
     for off in range(1, G):
         to = lax.rem(g + off, G)
@@ -661,6 +668,7 @@
             vmem((PHASES, members, R, T, V), f32),
             dma((PHASES, 2, M)), dma((PHASES, 2, M)), dma((G,)), dma((PHASES, T)),
             dma((PHASES, 9)), dma((PHASES, 9)), dma((PHASES, M)), dma((PHASES, M)), dma((3,)), dma((PHASES,)),
+            pltpu.SemaphoreType.REGULAR((2,)),
         ],
         compiler_params=pltpu.CompilerParams(
             collective_id=0, has_side_effects=True, vmem_limit_bytes=56 * 1024 * 1024

time: 64.9 us -> 61.9 us (0.954)
  Pallas kernels: 63.6 us -> 60.5 us
    pallas_call x1, Pallas kernels: 63.6 us -> 60.5 us  [local(): pl.pallas_call(functools.partial(kernel, (M, G, K, R, V, O)), out_shape=p...]
where the time goes in v2:
time: 61.9 us; the launch traced here: 61.7 us
  Pallas kernels  60.5 us (98%)
  local copies, waits for them, and re-layouts  1.15 us (2%)
    pallas_call x1, Pallas kernels, local(): pl.pallas_call(functools.partial(kernel, (M, G, K, R, V, O)), out_shape=p...  60.5 us

profile of v2, /device:TPU:33, one launch (start us, length us, event | category | flops | bytes accessed | tf_op | source)
XLA Modules:
  0.0 61.7 jit_solution(11442429127825517009)
XLA Ops:
  0.0 60.5 %shard_map.55 = f32[3,2,128,512]{3,2,1,0:T(8,128)S(1)} custom-call(f32[3,2,128,512]{3,2,1,0:T(8,128)} %ens_ref.1, f32[32,128]{1,0:T(8,128)} %bitcast.4, f32[32,128]{1,0:T(8,128)} %bitcast.5, s32[32,128]{1,0:T(8,128)} %bitcast.6, s32[1,32]{1,0:T(1,128)} %bitcast.7), custom_call_target="tpu_custom_call" | custom-call | tf_op jit(solution)/shard_map/pallas_call | solution.py:636
  60.5 1.1 %copy.7 = f32[3,2,128,512]{3,2,1,0:T(8,128)} copy(f32[3,2,128,512]{3,2,1,0:T(8,128)S(1)} %shard_map.55) | data formatting | bytes 3145728

commit v3 on v2

--- a/solution.py
+++ b/solution.py
@@ -41,8 +41,9 @@
     dims,
     ens_ref, value_any, error_any, index_any, count_ref, out_ref,
     value_ref, error_ref, index_ref, ens, pack, obs, slots, place, lochi, loclo, qhi, qlo, own, hin,
-    halo_out, row_in, side_in, root, inv, step, drv, half_ref, wt, xt, mean, outgoing,
+    halo_out, row_in, side_in, yfull, zfull, step, ypack, zpack, drv, half_ref, wt, xt, mean, outgoing, seam_tile, seam_out, seam_in,
     ens_send, ens_recv, obs_send, obs_recv, halo_send, halo_recv, out_send, out_recv, local_sem, own_sem, entry_sem,
+    seam_send, seam_recv,
 ):
     M, G, K, R, V, O = dims
     members = M * K
@@ -68,6 +69,8 @@
 
     for p in range(PHASES):
         own_copy(p).start()
+    seam_load = pltpu.make_async_copy(ens_ref.at[:, :, tile(1, 0), :], seam_tile, local_sem.at[3])
+    seam_load.start()
 
     column = m * G + g
     col_tile = column // T
@@ -90,14 +93,35 @@
     up_ok = g > 0
     down_ok = g < G - 1
     row_ok = {-1: up_ok, 1: down_ok}
+    seam_load.wait()
+    tiles = V // LANES
+    seam_rows = tiles * SUB
+    seam_out[...] = jnp.zeros(seam_out.shape, f32)
+    for i in range(R):
+        for k in range(K):
+            for t in range(tiles):
+                at = t * SUB + i * (SUB // R) + k
+                seam_out[at : at + 1, :] = seam_tile[k, i, 0:1, t * LANES : (t + 1) * LANES]
+
+    def seam_copy(source):
+        return pltpu.make_async_remote_copy(
+            src_ref=seam_out, dst_ref=seam_in.at[pl.ds(pl.multiple_of(source * seam_rows, SUB), seam_rows)],
+            send_sem=seam_send.at[0], recv_sem=seam_recv.at[source],
+            device_id=(0, g), device_id_type=MESH,
+        )
+
+    @pl.when(m == 0)
+    def _():
+        seam_in[:seam_rows, :] = seam_out[...]
+
     pl.semaphore_wait(barrier, len(x_peers) + len(y_peers) + len(z_peers))
     for peer in y_peers:
         pl.semaphore_signal(entry_sem.at[0], inc=1, device_id=peer, device_id_type=MESH)
 
-    pieces = ((0, 1), (1, K))
+    pieces = (((0, 2), (2, K)), ((0, 1), (1, K)))
 
     def ens_copy(p, n, off, to, at):
-        a, b = pieces[n]
+        a, b = pieces[p][n]
         return pltpu.make_async_remote_copy(
             src_ref=ens_ref.at[a:b, :, tile(p, to), :],
             dst_ref=ens.at[p, pl.ds(at * K + a, b - a)],
@@ -107,19 +131,15 @@
 
     order = [4, 5, 3, 2, 6, 1, 7]
     order = [off for off in order if off < M] + [off for off in range(1, M) if off not in order]
-    for n in range(2):
-        for off in order:
-            ens_copy(0, n, off, lax.rem(m + off, M), m).start()
+    @pl.when(m != 0)
+    def _():
+        seam_copy(m).start()
+
+    for off in order:
+        ens_copy(0, 0, off, lax.rem(m + off, M), m).start()
     pl.semaphore_wait(entry_sem.at[0], len(y_peers))
     for peer in x_peers:
         pl.semaphore_signal(entry_sem.at[1], inc=1, device_id=peer, device_id_type=MESH)
-    for off in order:
-        ens_copy(1, 0, off, lax.rem(m + off, M), m).start()
-    for off in order:
-        to = lax.rem(m + off, M)
-        @pl.when(to == 0)
-        def _():
-            ens_copy(1, 1, off, to, m).start()
 
     for load in loads:
         load.wait()
@@ -166,6 +186,9 @@
             pl.ds(pl.multiple_of(g * SUB, SUB), SUB), :
         ]
 
+    for p, n in ((0, 1), (1, 0)):
+        for off in order:
+            ens_copy(p, n, off, lax.rem(m + off, M), m).start()
     for s, (hm, hg) in enumerate(holders):
         @pl.when(jnp.logical_not(jnp.logical_and(hm == m, hg == g)))
         def _():
@@ -177,8 +200,6 @@
             for off in range(1, M):
                 came = lax.rem(m + M - off, M)
                 ens_copy(p, n, off, came, came).wait_recv()
-
-    tiles = V // LANES
 
     def gather(p):
         for i in range(R):
@@ -205,6 +226,35 @@
                 slots[i, k * T : (k + 1) * T, :] = wgt * (seen[k] - avg)
             slots[i, members * T : (members + 1) * T, :] = wgt * (val - avg)
 
+    def gather_seam():
+        for n in range(1, M):
+            seam_copy(n).wait_recv()
+        for i in range(R):
+            wgt = obs[1, i : i + 1, :]
+            val = obs[1, R + i : R + i + 1, :]
+            idx = obs[1, 2 * R + i : 2 * R + i + 1, :].astype(jnp.int32)
+            cell = idx & (CELLS - 1)
+            place[2 * i, 0:1, :] = (cell >> 4).astype(f32)
+            place[2 * i + 1, 0:1, :] = (cell & (SIDE - 1)).astype(f32)
+            wide = jnp.broadcast_to(idx, (M, O))
+            lane = wide & (LANES - 1)
+            which = wide >> 7
+            seen = []
+            for k in range(K):
+                got = None
+                for t in range(tiles):
+                    rows = seam_in[pl.ds(t * SUB + i * (SUB // R) + k, M, stride=seam_rows), :]
+                    more = jnp.take_along_axis(rows, lane, axis=1)
+                    got = more if got is None else jnp.where(which == t, more, got)
+                seen.append(got)
+            total = seen[0]
+            for k in range(1, K):
+                total = total + seen[k]
+            avg = jnp.sum(total, axis=0, keepdims=True) * (1.0 / members)
+            for k in range(K):
+                slots[i, pl.ds(k * T, M, stride=K * T), :] = wgt * (seen[k] - avg)
+            slots[i, members * T : members * T + 1, :] = wgt * (val - avg)
+
     sub8 = lax.broadcasted_iota(jnp.int32, (SUB, O), 0)
 
     def products(c, i):
@@ -324,26 +374,46 @@
     west = (lane & 32) == 0
     sub = lax.broadcasted_iota(jnp.int32, (SUB, OWN), 0)
 
-    def square(left, right, into, first):
+    front = lane < OWN // 2
+    row_in_block = sub - jnp.where(front, 0, SUB // 2)
+    quarter = SUB // 2
+
+    def pack_rows(kb, r, jb, full):
+        k = SUB * kb + r
+        one = full[k * members + SUB * jb : k * members + SUB * (jb + 1), :]
+        two = full[(k + quarter) * members + SUB * jb : (k + quarter) * members + SUB * (jb + 1), :]
+        return jnp.where(front, one, two)
+
+    def packed_at(kb, r, jb):
+        at = (quarter * kb + r) * members + SUB * jb
+        return slice(at, at + SUB)
+
+    def square(left, right, full, packed, first=False):
         for kb in range(blocks):
-            for k0 in range(kb * SUB, (kb + 1) * SUB, 4):
-                ks = range(k0, k0 + 4)
-                sums = {}
-                for i in range(members):
-                    rights = [right[i * members + SUB * jb : i * members + SUB * (jb + 1), :] for jb in range(kb, blocks)]
-                    for k in ks:
-                        lone = left[k * members + i : k * members + i + 1, :]
-                        for jb in range(kb, blocks):
-                            term = lone * rights[jb - kb]
-                            sums[k, jb] = term if i == 0 else sums[k, jb] + term
-                for k in ks:
+            sums = {}
+            for i in range(members):
+                rights = [right[i * members + SUB * jb : i * members + SUB * (jb + 1), :] for jb in range(kb, blocks)]
+                for r in range(quarter):
+                    at = (quarter * kb + r) * members + i
+                    lone = left[at : at + 1, :]
                     for jb in range(kb, blocks):
-                        out = sums[k, jb]
-                        if first:
-                            out = -0.5 * out
-                            if jb == kb:
-                                out = out + jnp.where(sub == k % SUB, 1.5, 0.0)
-                        put_entry(into, k, jb, out)
+                        term = lone * rights[jb - kb]
+                        sums[r, jb] = term if i == 0 else sums[r, jb] + term
+            for r in range(quarter):
+                for jb in range(kb, blocks):
+                    out = sums[r, jb]
+                    if first:
+                        out = -0.5 * out
+                        if jb == kb:
+                            out = out + jnp.where(row_in_block == r, 1.5, 0.0)
+                    swapped = pltpu.roll(out, OWN // 2, 1)
+                    put_entry(full, SUB * kb + r, jb, jnp.where(front, out, swapped))
+                    put_entry(full, SUB * kb + quarter + r, jb, jnp.where(front, swapped, out))
+                    if packed is not None:
+                        packed[packed_at(kb, r, jb), :] = out
+                if packed is not None:
+                    for jb in range(kb):
+                        packed[packed_at(kb, r, jb), :] = pack_rows(kb, r, jb, full)
 
     def put_entry(into, k, jb, out):
         into[k * members + SUB * jb : k * members + SUB * (jb + 1), :] = out
@@ -400,9 +470,10 @@
     def phase(p, carry):
         first_phase = p == 0
 
-        @pl.when(jnp.logical_or(first_phase, m > 0))
-        def _():
-            wait_ens(p)
+        for n in range(PHASES):
+            @pl.when(p == n)
+            def _():
+                wait_ens(n)
 
         gather(p)
         for c in range(T):
@@ -422,8 +493,7 @@
 
         @pl.when(jnp.logical_and(first_phase, m == 0))
         def _():
-            wait_ens(1)
-            gather(1)
+            gather_seam()
             edges = []
             for i in range(R):
                 products(0, i)
@@ -443,10 +513,7 @@
         @pl.when(first_phase)
         def _():
             for off in order:
-                to = lax.rem(m + off, M)
-                @pl.when(to != 0)
-                def _():
-                    ens_copy(1, 1, off, to, m).start()
+                ens_copy(1, 1, off, lax.rem(m + off, M), m).start()
 
         @pl.when(p > 0)
         def _():
@@ -516,7 +583,6 @@
             top = prec[row_of(SUB * b + SUB - 1, b) : row_of(SUB * b + SUB - 1, b) + SUB]
             last = prec[row_of(SUB * b + SUB - 2, b) : row_of(SUB * b + SUB - 2, b) + 1]
             drv[SUB * b : SUB * (b + 1), :] = jnp.where(sub < SUB - 1, top, last)
-        y0, y1, z0, z1 = root.at[0], root.at[1], inv.at[0], inv.at[1]
         inflate = (members - 1) / INFLATION_FACTOR
         for k in range(members):
             kb = k // SUB
@@ -527,41 +593,44 @@
                     if keep is not None:
                         out = jnp.where(keep, out, 0.0)
                     out = out + jnp.where(sub == k % SUB, inflate, 0.0)
-                put_entry(y1, k, jb, out)
+                put_entry(yfull, k, jb, out)
         for b in range(blocks):
             for e in (SUB - 1, SUB - 2):
                 k = SUB * b + e
-                y1[k * members + SUB * b : k * members + SUB * (b + 1), :] = y1[
+                yfull[k * members + SUB * b : k * members + SUB * (b + 1), :] = yfull[
                     pl.ds(SUB * b * members + k, SUB, stride=members), :
                 ]
         squares = None
         for n in range(members * blocks):
-            line = y1[n * SUB : (n + 1) * SUB, :]
+            line = yfull[n * SUB : (n + 1) * SUB, :]
             squares = line * line if squares is None else squares + line * line
         norm = jnp.sqrt(jnp.sum(squares, axis=0, keepdims=True))
         small = 1.0 / norm
         for k in range(members):
             for jb in range(blocks):
                 rows = slice(k * members + SUB * jb, k * members + SUB * (jb + 1))
-                start = y1[rows, :] * small
+                start = yfull[rows, :] * small
                 first_m = -0.5 * start
                 if jb == k // SUB:
                     first_m = first_m + jnp.where(sub == k % SUB, 1.5, 0.0)
-                y1[rows, :] = start
+                yfull[rows, :] = start
                 step[rows, :] = first_m
-                z0[rows, :] = first_m
-        square(y1, step, y0, False)
+        for kb in range(blocks):
+            for r in range(quarter):
+                for jb in range(blocks):
+                    ypack[packed_at(kb, r, jb), :] = pack_rows(kb, r, jb, yfull)
+                    zpack[packed_at(kb, r, jb), :] = pack_rows(kb, r, jb, step)
+        square(ypack, step, yfull, ypack)
 
         def sweep(n, carry):
-            now = lax.rem(n, 2)
-            square(inv.at[now], root.at[now], step, True)
-            square(root.at[now], step, root.at[1 - now], False)
-            square(inv.at[now], step, inv.at[1 - now], False)
+            square(zpack, yfull, step, None, True)
+            square(ypack, step, yfull, ypack)
+            square(zpack, step, zfull, zpack)
             return carry
 
         lax.fori_loop(0, NS_ITERS - 2, sweep, 0)
-        square(z0, y0, step, True)
-        square(z0, step, z1, False)
+        square(zpack, yfull, step, None, True)
+        square(zpack, step, zfull, None)
 
         shrink = 1.0 / jnp.sqrt(norm)
 
@@ -570,7 +639,7 @@
             for i in range(members):
                 lone = vector[i : i + 1, :]
                 for jb in range(blocks):
-                    term = lone * z1[i * members + SUB * jb : i * members + SUB * (jb + 1), :]
+                    term = lone * zfull[i * members + SUB * jb : i * members + SUB * (jb + 1), :]
                     sums[jb] = term if i == 0 else sums[jb] + term
             return [line * shrink for line in sums]
 
@@ -581,7 +650,7 @@
         for k in range(members):
             for jb in range(blocks):
                 wt[k, SUB * jb : SUB * (jb + 1), :] = (
-                    mean_w[jb] + spread * z1[k * members + SUB * jb : k * members + SUB * (jb + 1), :]
+                    mean_w[jb] + spread * zfull[k * members + SUB * jb : k * members + SUB * (jb + 1), :]
                 )
 
         return carry
@@ -604,6 +673,10 @@
     @pl.when(col_owner != m)
     def _():
         obs_copy(col_owner, g, g, col_phase, col_at).wait_send()
+
+    @pl.when(m != 0)
+    def _():
+        seam_copy(m).wait_send()
 
     for p in range(PHASES):
         for n in range(2):
@@ -657,18 +730,24 @@
             vmem((PHASES, 2 * ROW_HALO + 2 * SIDE_HALO, packed), f32),
             vmem((PHASES, 2, ROW_HALO, packed), f32),
             vmem((PHASES, 6, SIDE_HALO, packed), f32),
-            vmem((2, square, OWN), f32),
-            vmem((2, square, OWN), f32),
             vmem((square, OWN), f32),
+            vmem((square, OWN), f32),
+            vmem((square, OWN), f32),
+            vmem((square // 2, OWN), f32),
+            vmem((square // 2, OWN), f32),
             vmem((members, OWN), f32),
             vmem((members, OWN), f32),
             vmem((members, members, OWN), f32),
             vmem((members, SUB * SUB, OWN), f32),
             vmem((SUB * SUB, OWN), f32),
             vmem((PHASES, members, R, T, V), f32),
+            vmem((K, R, T, V), f32),
+            vmem((V // LANES * SUB, LANES), f32),
+            vmem((M * (V // LANES) * SUB, LANES), f32),
             dma((PHASES, 2, M)), dma((PHASES, 2, M)), dma((G,)), dma((PHASES, T)),
-            dma((PHASES, 9)), dma((PHASES, 9)), dma((PHASES, M)), dma((PHASES, M)), dma((3,)), dma((PHASES,)),
+            dma((PHASES, 9)), dma((PHASES, 9)), dma((PHASES, M)), dma((PHASES, M)), dma((4,)), dma((PHASES,)),
             pltpu.SemaphoreType.REGULAR((2,)),
+            dma((1,)), dma((M,)),
         ],
         compiler_params=pltpu.CompilerParams(
             collective_id=0, has_side_effects=True, vmem_limit_bytes=56 * 1024 * 1024

time: 61.9 us -> 56.7 us (0.916)
  Pallas kernels: 60.5 us -> 55.4 us
    pallas_call x1, Pallas kernels: 60.5 us -> 55.4 us  [local(): pl.pallas_call(functools.partial(kernel, (M, G, K, R, V, O)), out_shape=p...]
where the time goes in v3:
time: 56.7 us; the launch traced here: 56.6 us
  Pallas kernels  55.4 us (98%)
  local copies, waits for them, and re-layouts  1.15 us (2%)
    pallas_call x1, Pallas kernels, local(): pl.pallas_call(functools.partial(kernel, (M, G, K, R, V, O)), out_shape=p...  55.4 us
    unnamed x1, local copies, waits for them, and re-layouts  1.15 us

profile of v3, /device:TPU:33, one launch (start us, length us, event | category | flops | bytes accessed | tf_op | source)
XLA Modules:
  0.0 56.6 jit_solution(5102635184153574528)
XLA Ops:
  0.0 55.4 %shard_map.55 = f32[3,2,128,512]{3,2,1,0:T(8,128)S(1)} custom-call(f32[3,2,128,512]{3,2,1,0:T(8,128)} %ens_ref.1, f32[32,128]{1,0:T(8,128)} %bitcast.4, f32[32,128]{1,0:T(8,128)} %bitcast.5, s32[32,128]{1,0:T(8,128)} %bitcast.6, s32[1,32]{1,0:T(1,128)} %bitcast.7), custom_call_target="tpu_custom_call" | custom-call | tf_op jit(solution)/shard_map/pallas_call | solution.py:709
  55.4 1.1 %copy.7 = f32[3,2,128,512]{3,2,1,0:T(8,128)} copy(f32[3,2,128,512]{3,2,1,0:T(8,128)S(1)} %shard_map.55) | data formatting | bytes 3145728

commit v4 on v3

--- a/solution.py
+++ b/solution.py
@@ -41,7 +41,7 @@
     dims,
     ens_ref, value_any, error_any, index_any, count_ref, out_ref,
     value_ref, error_ref, index_ref, ens, pack, obs, slots, place, lochi, loclo, qhi, qlo, own, hin,
-    halo_out, row_in, side_in, yfull, zfull, step, ypack, zpack, drv, half_ref, wt, xt, mean, outgoing, seam_tile, seam_out, seam_in,
+    halo_out, row_in, side_in, yfull, zfull, step, ypack, zpack, drv, half_ref, wt, xt, mean, outgoing, seam_tile, seam_out, seam_in, seam_side,
     ens_send, ens_recv, obs_send, obs_recv, halo_send, halo_recv, out_send, out_recv, local_sem, own_sem, entry_sem,
     seam_send, seam_recv,
 ):
@@ -189,10 +189,15 @@
     for p, n in ((0, 1), (1, 0)):
         for off in order:
             ens_copy(p, n, off, lax.rem(m + off, M), m).start()
-    for s, (hm, hg) in enumerate(holders):
-        @pl.when(jnp.logical_not(jnp.logical_and(hm == m, hg == g)))
+    def wait_obs(s, also):
+        hm, hg = holders[s]
+
+        @pl.when(jnp.logical_and(also, jnp.logical_not(jnp.logical_and(hm == m, hg == g))))
         def _():
             obs_copy(hm, hg, g, s // T, s % T).wait_recv()
+
+    for s in range(T):
+        wait_obs(s, jnp.bool_(True))
 
     def wait_ens(p):
         own_copy(p).wait()
@@ -475,6 +480,8 @@
             def _():
                 wait_ens(n)
 
+        for s in range(T, PHASES * T):
+            wait_obs(s, jnp.logical_and(p == 1, m != 0) if s == T else p == 1)
         gather(p)
         for c in range(T):
             for i in range(R):
@@ -484,31 +491,16 @@
         own[...] = both[:, :OWN]
         halo_out[p] = jnp.transpose(both[:, OWN:])[: halo_out.shape[1]]
 
+
+        @pl.when(jnp.logical_and(first_phase, m == 0))
+        def _():
+            halo_out[0, 2 * ROW_HALO : 2 * ROW_HALO + SIDE_HALO, :] = seam_side[...]
+
         plans = [halo_plan(p, dm, dg) for dm, dg in near]
         for (dm, dg), (send, recv, outward, inward, landing) in zip(near, plans):
-            if dm >= 0:
-                @pl.when(send)
-                def _():
-                    outward().start()
-
-        @pl.when(jnp.logical_and(first_phase, m == 0))
-        def _():
-            gather_seam()
-            edges = []
-            for i in range(R):
-                products(0, i)
-                edges.append(edge_weight(0, i, row_weight(0, i), 1))
-            high, low = split(jnp.concatenate(edges, axis=1))
-            seam = qhi[:, : R * O]
-            halo_out[0, 2 * ROW_HALO : 2 * ROW_HALO + SIDE_HALO, :] = (
-                dot(high, seam) + dot(low, seam) + dot(high, qlo[:, : R * O])
-            )
-
-        for (dm, dg), (send, recv, outward, inward, landing) in zip(near, plans):
-            if dm < 0:
-                @pl.when(send)
-                def _():
-                    outward().start()
+            @pl.when(send)
+            def _():
+                outward().start()
 
         @pl.when(first_phase)
         def _():
@@ -628,7 +620,7 @@
             square(zpack, step, zfull, zpack)
             return carry
 
-        lax.fori_loop(0, NS_ITERS - 2, sweep, 0)
+        lax.fori_loop(0, NS_ITERS - 2, sweep, 0, unroll=True)
         square(zpack, yfull, step, None, True)
         square(zpack, step, zfull, None)
 
@@ -662,6 +654,19 @@
             send_sem=out_send.at[p, away], recv_sem=out_recv.at[p, away],
             device_id=(dest, g), device_id_type=MESH,
         )
+
+    wait_obs(T, m == 0)
+
+    @pl.when(m == 0)
+    def _():
+        gather_seam()
+        edges = []
+        for i in range(R):
+            products(0, i)
+            edges.append(edge_weight(0, i, row_weight(0, i), 1))
+        high, low = split(jnp.concatenate(edges, axis=1))
+        seam = qhi[:, : R * O]
+        seam_side[...] = dot(high, seam) + dot(low, seam) + dot(high, qlo[:, : R * O])
 
     lax.fori_loop(0, PHASES, phase, 0)
     results(PHASES - 1)
@@ -744,6 +749,7 @@
             vmem((K, R, T, V), f32),
             vmem((V // LANES * SUB, LANES), f32),
             vmem((M * (V // LANES) * SUB, LANES), f32),
+            vmem((SIDE_HALO, packed), f32),
             dma((PHASES, 2, M)), dma((PHASES, 2, M)), dma((G,)), dma((PHASES, T)),
             dma((PHASES, 9)), dma((PHASES, 9)), dma((PHASES, M)), dma((PHASES, M)), dma((4,)), dma((PHASES,)),
             pltpu.SemaphoreType.REGULAR((2,)),

time: 56.7 us -> 56.1 us (0.989)
  Pallas kernels: 55.4 us -> 54.8 us
    pallas_call x1, Pallas kernels: 55.4 us -> 54.8 us  [local(): pl.pallas_call(functools.partial(kernel, (M, G, K, R, V, O)), out_shape=p...]
where the time goes in v4:
time: 56.1 us; the launch traced here: 56 us
  Pallas kernels  54.8 us (98%)
  local copies, waits for them, and re-layouts  1.15 us (2%)
    pallas_call x1, Pallas kernels, local(): pl.pallas_call(functools.partial(kernel, (M, G, K, R, V, O)), out_shape=p...  54.8 us
    unnamed x1, local copies, waits for them, and re-layouts  1.15 us

profile of v4, /device:TPU:33, one launch (start us, length us, event | category | flops | bytes accessed | tf_op | source)
XLA Modules:
  0.0 56.0 jit_solution(5454538110599164308)
XLA Ops:
  0.0 54.8 %shard_map.55 = f32[3,2,128,512]{3,2,1,0:T(8,128)S(1)} custom-call(f32[3,2,128,512]{3,2,1,0:T(8,128)} %ens_ref.1, f32[32,128]{1,0:T(8,128)} %bitcast.4, f32[32,128]{1,0:T(8,128)} %bitcast.5, s32[32,128]{1,0:T(8,128)} %bitcast.6, s32[1,32]{1,0:T(1,128)} %bitcast.7), custom_call_target="tpu_custom_call" | custom-call | tf_op jit(solution)/shard_map/pallas_call | solution.py:714
  54.8 1.1 %copy.7 = f32[3,2,128,512]{3,2,1,0:T(8,128)} copy(f32[3,2,128,512]{3,2,1,0:T(8,128)S(1)} %shard_map.55) | data formatting | bytes 3145728

commit v5 on v4

--- a/solution.py
+++ b/solution.py
@@ -457,17 +457,17 @@
                                 lanes = f * CELLS + h * LANES
                                 outgoing[p, k0 + pair + e, i, :, lanes : lanes + LANES] = turned[at : at + T]
                                 at += T
-            for core in range(2):
-                dest = 2 * chip + core
-                away = lax.rem(dest - m + M, M)
-
-                @pl.when(away != 0)
-                def _():
-                    out_copy(p, away, dest, m).start()
-
-                @pl.when(away == 0)
-                def _():
-                    out_ref[:, :, tile(p, m), :] = outgoing[p, pl.ds(dest * K, K)]
+                for core in ((), (0,), (1,))[pair // 2]:
+                    dest = 2 * chip + core
+                    away = lax.rem(dest - m + M, M)
+
+                    @pl.when(away != 0)
+                    def _():
+                        out_copy(p, away, dest, m).start()
+
+                    @pl.when(away == 0)
+                    def _():
+                        out_ref[:, :, tile(p, m), :] = outgoing[p, pl.ds(dest * K, K)]
             return carry
 
         lax.fori_loop(0, chips, update, 0)

time: 56.1 us -> 56.1 us (level)
  no operation moved by 1% of the time
where the time goes in v5:
time: 56.1 us; the launch traced here: 56 us
  Pallas kernels  54.8 us (98%)
  local copies, waits for them, and re-layouts  1.15 us (2%)
    pallas_call x1, Pallas kernels, local(): pl.pallas_call(functools.partial(kernel, (M, G, K, R, V, O)), out_shape=p...  54.8 us
    unnamed x1, local copies, waits for them, and re-layouts  1.15 us

profile of v5, /device:TPU:33, one launch (start us, length us, event | category | flops | bytes accessed | tf_op | source)
XLA Modules:
  0.0 56.0 jit_solution(10513656865693779421)
XLA Ops:
  0.0 54.8 %shard_map.55 = f32[3,2,128,512]{3,2,1,0:T(8,128)S(1)} custom-call(f32[3,2,128,512]{3,2,1,0:T(8,128)} %ens_ref.1, f32[32,128]{1,0:T(8,128)} %bitcast.4, f32[32,128]{1,0:T(8,128)} %bitcast.5, s32[32,128]{1,0:T(8,128)} %bitcast.6, s32[1,32]{1,0:T(1,128)} %bitcast.7), custom_call_target="tpu_custom_call" | custom-call | tf_op jit(solution)/shard_map/pallas_call | solution.py:714
  54.8 1.1 %copy.7 = f32[3,2,128,512]{3,2,1,0:T(8,128)} copy(f32[3,2,128,512]{3,2,1,0:T(8,128)S(1)} %shard_map.55) | data formatting | bytes 3145728
